TPU v7x, 32 devices: a whole 2x2x4 slice. The times are simulated.
32 devices in a mesh: blk: 16 (over z, y, core), dp: 2 (over x).
Axes of the slice: x: 2, y: 2, z: 4, core: 2. Of those that a mesh axis runs over, the one named last changes fastest.
Arguments:
- query_feats: bfloat16 [2, 6144, 1024], P('dp', 'blk'), may hold values from -12 to 12
- item_feats: bfloat16 [2, 6144, 1024], P('dp', 'blk'), may hold values from -12 to 12
- item_ids: int32 [2, 6144], P('dp', 'blk'), may hold values from 0 to 1048575
- bucket_ids: int32 [2, 6144], P('dp', 'blk'), may hold values from 0 to 255
- bucket_logq: float32 [256], replicated, may hold values from -7 to -5.5
- query_tower: bfloat16 [1024, 256], replicated, may hold values from -0.1875 to 0.1875
- item_tower: bfloat16 [1024, 256], replicated, may hold values from -0.1875 to 0.1875
Outputs:
- grad_query_tower: float32 [1024, 256], replicated
- grad_item_tower: float32 [1024, 256], replicated
- loss: float32 [], replicated
All inputs are finite; a program needn't handle non-finite values.
Results may differ from a plain program's by a relative error of at most 0.0041.
Values may be sent and summed in bfloat16 or wider, within the bound.
A program may use at most 128 MiB of HBM per device.

v0:
```python
import math
import jax
import jax.numpy as jnp
from jax import lax
from jax.sharding import PartitionSpec as P

EXCLUDED = -1e30


def contract_last(left, right):
    return lax.dot_general(
        left, right, (((1,), (1,)), ((), ())), preferred_element_type=jnp.float32
    )


def contract_first(left, right):
    return lax.dot_general(
        left, right, (((0,), (0,)), ((), ())), preferred_element_type=jnp.float32
    )


def on_device(query_feats, item_feats, item_ids, bucket_ids, bucket_logq, query_tower, item_tower):
    query_input = query_feats[0]
    item_input = item_feats[0]
    own_ids = item_ids[0]
    local_rows = query_input.shape[0]
    embed_width = query_tower.shape[1]
    scaling = 1.0 / math.sqrt(embed_width)
    query_vecs = jnp.dot(query_input, query_tower, preferred_element_type=jnp.float32).astype(
        jnp.bfloat16
    )
    item_vecs = jnp.dot(item_input, item_tower, preferred_element_type=jnp.float32).astype(
        jnp.bfloat16
    )
    all_items = lax.all_gather(item_vecs, "blk", axis=0, tiled=True)
    all_ids, all_buckets = (
        lax.all_gather(own_ids, "blk", axis=0, tiled=True),
        lax.all_gather(bucket_ids[0], "blk", axis=0, tiled=True),
    )
    group_size = all_ids.shape[0]
    bucket_range = jnp.arange(bucket_logq.shape[0], dtype=jnp.int32)
    correction = jnp.sum(
        jnp.where(all_buckets[:, None] == bucket_range[None, :], bucket_logq[None, :], 0.0), axis=1
    )
    offset = lax.axis_index("blk") * local_rows
    rows_global = offset + jnp.arange(local_rows, dtype=jnp.int32)
    columns = jnp.arange(group_size, dtype=jnp.int32)
    scores = contract_last(query_vecs, all_items) * scaling - correction[None, :]
    duplicate = (all_ids[None, :] == own_ids[:, None]) & (columns[None, :] != rows_global[:, None])
    masked = jnp.where(duplicate, EXCLUDED, scores)
    peaks = jnp.max(masked, axis=1)
    log_total = peaks + jnp.log(jnp.sum(jnp.exp(masked - peaks[:, None]), axis=1))
    softmax = jnp.exp(masked - log_total[:, None]).astype(jnp.bfloat16)
    positive = jnp.diagonal(lax.dynamic_slice_in_dim(scores, offset, local_rows, 1))
    loss_local = jnp.sum(log_total - positive)
    query_grad = (
        (
            jnp.dot(softmax, all_items, preferred_element_type=jnp.float32)
            - item_vecs.astype(jnp.float32)
        )
        * scaling
    ).astype(jnp.bfloat16)
    tower_query = contract_first(query_input, query_grad)
    all_totals = lax.all_gather(log_total, "blk", axis=0, tiled=True)
    own_correction = lax.dynamic_slice_in_dim(correction, offset, local_rows, 0)
    shard_rows = lax.all_gather(query_vecs, "blk", axis=0, tiled=True)
    row_count = shard_rows.shape[0]
    piece_rows = jnp.arange(row_count, dtype=jnp.int32)
    piece_scores = contract_last(shard_rows, item_vecs) * scaling - own_correction[None, :]
    piece_dup = (own_ids[None, :] == all_ids[:, None]) & (
        rows_global[None, :] != piece_rows[:, None]
    )
    piece_masked = jnp.where(piece_dup, EXCLUDED, piece_scores)
    piece_soft = jnp.exp(piece_masked - all_totals[:, None]).astype(jnp.bfloat16)
    item_sums = contract_first(piece_soft, shard_rows)
    item_grad = ((item_sums - query_vecs.astype(jnp.float32)) * scaling).astype(jnp.bfloat16)
    tower_item = contract_first(item_input, item_grad)
    grad_query, grad_item, loss_total = lax.psum(
        (tower_query, tower_item, loss_local), ("blk", "dp")
    )
    loss = loss_total / (lax.axis_size("dp") * group_size)
    return (grad_query, grad_item, loss)


def solution(mesh):
    return jax.shard_map(
        on_device,
        mesh=mesh,
        in_specs=(
            P("dp", "blk", None),
            P("dp", "blk", None),
            P("dp", "blk"),
            P("dp", "blk"),
            P(),
            P(),
            P(),
        ),
        out_specs=(P(), P(), P()),
        check_vma=False,
    )
```

profile of v0, /device:TPU:0, one launch (start us, length us, event | category | flops | bytes accessed | tf_op | source)
XLA Modules:
  0.0 271.1 jit_solution(16974433415751441784)
XLA Ops:
  7.2 0.0 copy-start
  7.2 0.0 all-gather.6.cloned.1.call-start
  7.2 1.1 copy-done
  8.3 2.1 convolution_convert_fusion
  10.4 0.0 all-gather.6.cloned.1.call-update
  10.4 0.0 all-gather.8.cloned.1.call-start
  10.5 2.3 convolution_convert_fusion.1
  12.8 0.0 all-gather.8.cloned.1.call-update
  12.8 0.0 all-reduce.3.cloned.1.call-start
  12.9 0.7 reduce
  13.6 23.4 %all-gather.1 = s32[1,6144]{1,0:T(1,128)S(1)} all-gather(s32[1,384]{1,0:T(1,128)} %param.10), channel_id=3, replica_groups=mesh['blk'=16,'dp'=2] {'blk'}, dimensions={1}, use_global_device_ids=true | all-gather | bytes 26112 | tf_op jit(solution)/shard_map/all_gather | solution.py:38
  37.0 4.4 %select_reduce_fusion = f32[6144]{0:T(1024)S(1)} fusion(f32[256]{0:T(256)} %param.11, s32[6144]{0:T(1024)S(1)} %bitcast.30), kind=kLoop, calls=%fused_computation.10 | loop fusion | flops 4712448 | bytes 50176 | tf_op jit(solution)/shard_map/reduce_sum | solution.py:42
  41.4 0.1 dynamic_slice.6
  41.5 18.0 %all-gather = s32[1,6144]{1,0:T(1,128)S(1)} all-gather(s32[1,384]{1,0:T(1,128)} %param.9), channel_id=2, replica_groups=mesh['blk'=16,'dp'=2] {'blk'}, dimensions={1}, use_global_device_ids=true | all-gather | bytes 26112 | tf_op jit(solution)/shard_map/all_gather | solution.py:37
  59.5 0.0 all-gather.6.cloned.1.call-done
  59.5 5.1 %fusion.3 = (f32[384]{0:T(512)S(1)}, f32[384,6144]{1,0:T(8,128)S(1)}) fusion(s32[384]{0:T(512)S(1)} %iota_add_fusion, s32[6144]{0:T(1024)S(1)} %bitcast.26, s32[384]{0:T(512)S(1)} %reduce, f32[6144]{0:T(1024)S(1)} %select_reduce_fusion, bf16[384,256]{1,0:T(8,128)(2,1)} %convolution_convert_fusion.1, bf16[6144,256]{1,0:T(8,128)(2,1)} %all-gather.6.cloned.1.call-done), kind=kOutput, calls=%fused_computation.12 | convolution fusion | flops 1224474240 | bytes 12833280 | tf_op jit(solution)/shard_map/dot_general | solution.py:11
  64.6 0.0 copy-start.1
  64.6 0.0 copy-start.3
  64.6 0.0 copy-start.4
  64.6 3.6 %copy-done.1 = f32[384,6144]{1,0:T(8,128)} copy-done((f32[384,6144]{1,0:T(8,128)}, f32[384,6144]{1,0:T(8,128)S(1)}, u32[]{:S(2)}) %copy-start.1) | copy-done | bytes 9437208
  68.2 0.1 constant_dynamic-slice_fusion
  68.3 3.4 %gather_fusion = f32[384]{0:T(512)S(1)} fusion(f32[384,384]{1,0:T(8,128)S(1)} %constant_dynamic-slice_fusion, s32[384]{0:T(512)S(1)} %or_reduce_fusion), kind=kCustom, calls=%fused_computation | custom fusion | bytes 6144 | tf_op jit(solution)/shard_map/jit(diagonal)/cond/branch_0_fun/gather | solution.py:54
  71.7 6.0 %exponential_reduce_fusion = f32[384]{0:T(512)S(1)} fusion(f32[384,6144]{1,0:T(8,128)} %copy-done.1, f32[384]{0:T(512)S(1)} %get-tuple-element.19, s32[384]{0:T(512)S(1)} %iota_add_fusion, s32[6144]{0:T(1024)S(1)} %bitcast.27, s32[384]{0:T(512)S(1)} %reduce), kind=kLoop, calls=%fused_computation.4 | loop fusion | flops 14155392 | bytes 9467904 | tf_op jit(solution)/shard_map/reduce_sum | solution.py:52
  77.7 0.6 subtract_reduce_fusion
  78.3 19.5 %all-gather.2 = f32[16,1,384]{2,1,0:T(1,128)S(1)} all-gather(f32[1,1,384]{2,1,0:T(1,128)S(1)} %reshape.37), channel_id=1, replica_groups=mesh['blk'=16,'dp'=2] {'blk'}, dimensions={0}, use_global_device_ids=true | all-gather | bytes 26112 | tf_op jit(solution)/shard_map/all_gather | solution.py:64
  97.8 8.1 %all-gather.8.cloned.1.call-done = bf16[6144,256]{1,0:T(8,128)(2,1)} async-done(((bf16[384,256]{1,0:T(8,128)(2,1)}), bf16[6144,256]{1,0:T(8,128)(2,1)}) %all-gather.8.cloned.1.call-update) | async-done | bytes 3145744 | tf_op jit(solution)/shard_map/all_gather | solution.py:66
  105.9 0.0 copy-done.3
  105.9 0.0 copy-done.4
  105.9 0.0 copy-start.2
  105.9 8.5 %fusion.11 = bf16[384,256]{1,0:T(8,128)(2,1)S(1)} fusion(bf16[6144,256]{1,0:T(8,128)(2,1)} %all-gather.8.cloned.1.call-done, bf16[384,256]{1,0:T(8,128)(2,1)S(1)} %copy-done.3, f32[6144]{0:T(1024)S(1)} %bitcast.31, f32[384]{0:T(512)S(1)} %dynamic_slice.6, s32[384]{0:T(512)S(1)} %iota_add_fusion, s32[384]{0:T(512)S(1)} %reduce, s32[6144]{0:T(1024)S(1)} %bitcast.28, ...), kind=kOutput, calls=%fused_computation.24 | convolution fusion | flops 2435186688 | bytes 3789312 | tf_op jit(solution)/shard_map/dot_general | solution.py:17
  114.4 1.4 convolution_bitcast_fusion
  115.8 0.0 copy-done.2
  115.8 9.0 %convolution_bitcast_fusion.1 = f32[1024,256]{0,1:T(8,128)} fusion(bf16[6144,256]{1,0:T(8,128)(2,1)} %all-gather.6.cloned.1.call-done, f32[384,6144]{1,0:T(8,128)} %copy-done.1, f32[384]{0:T(512)S(1)} %get-tuple-element.18, s32[384]{0:T(512)S(1)} %iota_add_fusion, s32[6144]{0:T(1024)S(1)} %bitcast.29, s32[384]{0:T(512)S(1)} %reduce, ...), kind=kOutput, calls=%fused_computation.16 | convolution fusion | flops 1423835136 | bytes 14643712 | tf_op jit(solution)/shard_map/dot_general | solution.py:17
  124.8 0.0 all-reduce.3.cloned.1.call-update
  124.9 39.8 %psum.23 = f32[]{:T(128)} all-reduce(f32[]{:T(128)} %get-tuple-element.17), channel_id=1, replica_groups=mesh['blk'=16,'dp'=2] {'blk','dp'}, use_global_device_ids=true, to_apply=%region_6.7 | all-reduce | flops 1 | bytes 8 | tf_op jit(solution)/shard_map/psum | solution.py:78
  165.3 93.1 %all-reduce.3.cloned.1.call-done = (f32[1024,256]{0,1:T(8,128)}, f32[1024,256]{0,1:T(8,128)}) async-done(((f32[1024,256]{0,1:T(8,128)}, f32[1024,256]{0,1:T(8,128)}), (f32[1024,256]{0,1:T(8,128)}, f32[1024,256]{0,1:T(8,128)})) %all-reduce.3.cloned.1.call-update) | async-done | bytes 2097168 | tf_op jit(solution)/shard_map/psum | solution.py:78
  258.4 2.5 copy.16
  260.9 2.5 copy.17
  (3 shorter events, 0.0 us)
Async XLA Ops:
  7.2 1.1 copy-start
  7.2 52.3 %all-gather.6.cloned.1.call-start = ((), (), s32[]{:S(2)}) async-start(), calls=%async_computation | async-start | bytes 3342336 | tf_op jit(solution)/shard_map/all_gather | solution.py:35
  10.4 95.5 %all-gather.8.cloned.1.call-start = ((), (), s32[]{:S(2)}) async-start(), calls=%async_computation.1 | async-start | bytes 3342336 | tf_op jit(solution)/shard_map/all_gather | solution.py:66
  12.8 245.6 %all-reduce.3.cloned.1.call-start = ((), (), s32[]{:S(2)}) async-start(), calls=%async_computation.2 | async-start | bytes 4194304 | tf_op jit(solution)/shard_map/psum | solution.py:78
  64.6 3.6 %copy-start.1 = (f32[384,6144]{1,0:T(8,128)}, f32[384,6144]{1,0:T(8,128)S(1)}, u32[]{:S(2)}) copy-start(f32[384,6144]{1,0:T(8,128)S(1)} %get-tuple-element.20) | copy-start | bytes 28311556
  64.6 41.3 %copy-start.3 = (bf16[384,256]{1,0:T(8,128)(2,1)S(1)}, bf16[384,256]{1,0:T(8,128)(2,1)}, u32[]{:S(2)}) copy-start(bf16[384,256]{1,0:T(8,128)(2,1)} %convolution_convert_fusion) | copy-start | bytes 589828
  64.6 41.3 %copy-start.4 = (bf16[384,256]{1,0:T(8,128)(2,1)S(1)}, bf16[384,256]{1,0:T(8,128)(2,1)}, u32[]{:S(2)}) copy-start(bf16[384,256]{1,0:T(8,128)(2,1)} %convolution_convert_fusion.1) | copy-start | bytes 589828
  105.9 9.9 %copy-start.2 = (bf16[1,384,1024]{2,1,0:T(8,128)(2,1)S(1)}, bf16[1,384,1024]{2,1,0:T(8,128)(2,1)}, u32[]{:S(2)}) copy-start(bf16[1,384,1024]{2,1,0:T(8,128)(2,1)} %param.7) | copy-start | bytes 2359300
Sparse Core Ops, SparseCore 0:
  10.8 48.2 all-gather.5
  62.0 43.8 all-gather.7
  125.0 133.3 all-reduce.2
where the time goes:
time: 272 us; the launch traced here: 271 us
  waiting for transfers between devices  101 us (37%)
  blocking collectives  101 us (37%)
  matrix products  28.4 us (10%)
  between operations  15.6 us (6%)
  local copies, waits for them, and re-layouts  13.3 us (5%)
  other arithmetic  11.7 us (4%)
    psum x1, waiting for transfers between devices, on_device(): lax.psum((tower_query, tower_item, loss_local), ('blk', 'dp'))  93.1 us
    psum x1, blocking collectives, on_device(): lax.psum((tower_query, tower_item, loss_local), ('blk', 'dp'))  39.8 us
    all_gather x1, blocking collectives, on_device(): lax.all_gather(bucket_ids[0], 'blk', axis=0, tiled=True)  23.4 us
    all_gather x1, blocking collectives, on_device(): all_totals = lax.all_gather(log_total, 'blk', axis=0, tiled=True)  19.5 us
    dot_general x3, matrix products, contract_first(): lax.dot_general(left, right, (((0,), (0,)), ((), ())), preferred_element_...  18.9 us
    all_gather x1, blocking collectives, on_device(): lax.all_gather(own_ids, 'blk', axis=0, tiled=True)  18 us
    unnamed x13, local copies, waits for them, and re-layouts  9.76 us
    all_gather x1, waiting for transfers between devices, on_device(): shard_rows = lax.all_gather(query_vecs, 'blk', axis=0, tiled=True)  8.09 us
  transfers between devices with their start and end apart: 3, of which 2 were waited for; matrix products, arithmetic and copies ran while one was open for 8% of the time, Pallas kernels for 0%

commit v1 on v0

--- a/solution.py
+++ b/solution.py
@@ -5,6 +5,11 @@
 from jax.sharding import PartitionSpec as P
 
 EXCLUDED = -1e30
+
+
+def one_after_other(value, one, other):
+    half = lax.psum(value, one)
+    return lax.psum(half, other)
 
 
 def contract_last(left, right):
@@ -75,8 +80,8 @@
     item_sums = contract_first(piece_soft, shard_rows)
     item_grad = ((item_sums - query_vecs.astype(jnp.float32)) * scaling).astype(jnp.bfloat16)
     tower_item = contract_first(item_input, item_grad)
-    grad_query, grad_item, loss_total = lax.psum(
-        (tower_query, tower_item, loss_local), ("blk", "dp")
+    grad_query, grad_item, loss_total = one_after_other(
+        (tower_query, tower_item, loss_local), "dp", "blk"
     )
     loss = loss_total / (lax.axis_size("dp") * group_size)
     return (grad_query, grad_item, loss)

time: 272 us -> 301 us (1.11)
  waiting for transfers between devices: 101 us -> 132 us
    psum x1 -> x2, waiting for transfers between devices: 93.1 us -> 124 us  [the longest x1 62.5 us: one_after_other(): return lax.psum(half, other)]
    psum x1 -> x2, blocking collectives: 39.8 us -> 38.7 us  [the longest x1 33.2 us: one_after_other(): return lax.psum(half, other)]
  transfers between devices with their start and end apart: 3 -> 4, of which waited for: 2 -> 3; matrix products, arithmetic and copies ran while one was open for 8% -> 8% of each run, Pallas kernels for 0% -> 0%
where the time goes in v1:
time: 301 us
  waiting for transfers between devices  132 us (44%)
  blocking collectives  99.7 us (33%)
  matrix products  28.4 us (9%)
  between operations  15.6 us (5%)
  local copies, waits for them, and re-layouts  13.3 us (4%)
  other arithmetic  11.7 us (4%)
    psum x1, waiting for transfers between devices, one_after_other(): return lax.psum(half, other)  62.5 us
    psum x1, waiting for transfers between devices, one_after_other(): half = lax.psum(value, one)  61.4 us
    psum x1, blocking collectives, one_after_other(): return lax.psum(half, other)  33.2 us
    all_gather x1, blocking collectives, on_device(): lax.all_gather(bucket_ids[0], 'blk', axis=0, tiled=True)  23.4 us
    all_gather x1, blocking collectives, on_device(): all_totals = lax.all_gather(log_total, 'blk', axis=0, tiled=True)  19.5 us
    dot_general x3, matrix products, contract_first(): lax.dot_general(left, right, (((0,), (0,)), ((), ())), preferred_element_...  18.9 us
    all_gather x1, blocking collectives, on_device(): lax.all_gather(own_ids, 'blk', axis=0, tiled=True)  18 us
    unnamed x13, local copies, waits for them, and re-layouts  9.76 us
  transfers between devices with their start and end apart: 4, of which 3 were waited for; matrix products, arithmetic and copies ran while one was open for 8% of the time, Pallas kernels for 0%

profile of v1, /device:TPU:0, one launch (start us, length us, event | category | flops | bytes accessed | tf_op | source)
XLA Modules:
  0.0 300.9 jit_solution(2312098372734600482)
XLA Ops:
  7.2 0.0 copy-start
  7.2 0.0 all-gather.6.cloned.1.call-start
  7.2 1.1 copy-done
  8.3 2.1 convolution_convert_fusion
  10.4 0.0 all-gather.6.cloned.1.call-update
  10.4 0.0 all-gather.8.cloned.1.call-start
  10.5 2.3 convolution_convert_fusion.1
  12.8 0.0 all-gather.8.cloned.1.call-update
  12.8 0.0 all-reduce.7.cloned.1.call-start
  12.9 0.7 reduce
  13.6 23.4 %all-gather.1 = s32[1,6144]{1,0:T(1,128)S(1)} all-gather(s32[1,384]{1,0:T(1,128)} %param.10), channel_id=3, replica_groups=mesh['blk'=16,'dp'=2] {'blk'}, dimensions={1}, use_global_device_ids=true | all-gather | bytes 26112 | tf_op jit(solution)/shard_map/all_gather | solution.py:43
  37.0 4.4 %select_reduce_fusion = f32[6144]{0:T(1024)S(1)} fusion(f32[256]{0:T(256)} %param.11, s32[6144]{0:T(1024)S(1)} %bitcast.30), kind=kLoop, calls=%fused_computation.10 | loop fusion | flops 4712448 | bytes 50176 | tf_op jit(solution)/shard_map/reduce_sum | solution.py:47
  41.4 0.1 dynamic_slice.6
  41.5 18.0 %all-gather = s32[1,6144]{1,0:T(1,128)S(1)} all-gather(s32[1,384]{1,0:T(1,128)} %param.9), channel_id=2, replica_groups=mesh['blk'=16,'dp'=2] {'blk'}, dimensions={1}, use_global_device_ids=true | all-gather | bytes 26112 | tf_op jit(solution)/shard_map/all_gather | solution.py:42
  59.5 0.0 all-gather.6.cloned.1.call-done
  59.5 5.1 %fusion.3 = (f32[384]{0:T(512)S(1)}, f32[384,6144]{1,0:T(8,128)S(1)}) fusion(s32[384]{0:T(512)S(1)} %iota_add_fusion, s32[6144]{0:T(1024)S(1)} %bitcast.26, s32[384]{0:T(512)S(1)} %reduce, f32[6144]{0:T(1024)S(1)} %select_reduce_fusion, bf16[384,256]{1,0:T(8,128)(2,1)} %convolution_convert_fusion.1, bf16[6144,256]{1,0:T(8,128)(2,1)} %all-gather.6.cloned.1.call-done), kind=kOutput, calls=%fused_computation.12 | convolution fusion | flops 1224474240 | bytes 12833280 | tf_op jit(solution)/shard_map/dot_general | solution.py:16
  64.6 0.0 copy-start.1
  64.6 0.0 copy-start.3
  64.6 0.0 copy-start.4
  64.6 3.6 %copy-done.1 = f32[384,6144]{1,0:T(8,128)} copy-done((f32[384,6144]{1,0:T(8,128)}, f32[384,6144]{1,0:T(8,128)S(1)}, u32[]{:S(2)}) %copy-start.1) | copy-done | bytes 9437208
  68.2 0.1 constant_dynamic-slice_fusion
  68.3 3.4 %gather_fusion = f32[384]{0:T(512)S(1)} fusion(f32[384,384]{1,0:T(8,128)S(1)} %constant_dynamic-slice_fusion, s32[384]{0:T(512)S(1)} %or_reduce_fusion), kind=kCustom, calls=%fused_computation | custom fusion | bytes 6144 | tf_op jit(solution)/shard_map/jit(diagonal)/cond/branch_0_fun/gather | solution.py:59
  71.7 6.0 %exponential_reduce_fusion = f32[384]{0:T(512)S(1)} fusion(f32[384,6144]{1,0:T(8,128)} %copy-done.1, f32[384]{0:T(512)S(1)} %get-tuple-element.21, s32[384]{0:T(512)S(1)} %iota_add_fusion, s32[6144]{0:T(1024)S(1)} %bitcast.27, s32[384]{0:T(512)S(1)} %reduce), kind=kLoop, calls=%fused_computation.4 | loop fusion | flops 14155392 | bytes 9467904 | tf_op jit(solution)/shard_map/reduce_sum | solution.py:57
  77.7 0.6 subtract_reduce_fusion
  78.3 19.5 %all-gather.2 = f32[16,1,384]{2,1,0:T(1,128)S(1)} all-gather(f32[1,1,384]{2,1,0:T(1,128)S(1)} %reshape.37), channel_id=1, replica_groups=mesh['blk'=16,'dp'=2] {'blk'}, dimensions={0}, use_global_device_ids=true | all-gather | bytes 26112 | tf_op jit(solution)/shard_map/all_gather | solution.py:69
  97.8 8.1 %all-gather.8.cloned.1.call-done = bf16[6144,256]{1,0:T(8,128)(2,1)} async-done(((bf16[384,256]{1,0:T(8,128)(2,1)}), bf16[6144,256]{1,0:T(8,128)(2,1)}) %all-gather.8.cloned.1.call-update) | async-done | bytes 3145744 | tf_op jit(solution)/shard_map/all_gather | solution.py:71
  105.9 0.0 copy-done.3
  105.9 0.0 copy-done.4
  105.9 0.0 copy-start.2
  105.9 8.5 %fusion.11 = bf16[384,256]{1,0:T(8,128)(2,1)S(1)} fusion(bf16[6144,256]{1,0:T(8,128)(2,1)} %all-gather.8.cloned.1.call-done, bf16[384,256]{1,0:T(8,128)(2,1)S(1)} %copy-done.3, f32[6144]{0:T(1024)S(1)} %bitcast.31, f32[384]{0:T(512)S(1)} %dynamic_slice.6, s32[384]{0:T(512)S(1)} %iota_add_fusion, s32[384]{0:T(512)S(1)} %reduce, s32[6144]{0:T(1024)S(1)} %bitcast.28, ...), kind=kOutput, calls=%fused_computation.24 | convolution fusion | flops 2435186688 | bytes 3789312 | tf_op jit(solution)/shard_map/dot_general | solution.py:22
  114.4 1.4 convolution_bitcast_fusion
  115.8 0.0 copy-done.2
  115.8 9.0 %convolution_bitcast_fusion.1 = f32[1024,256]{0,1:T(8,128)} fusion(bf16[6144,256]{1,0:T(8,128)(2,1)} %all-gather.6.cloned.1.call-done, f32[384,6144]{1,0:T(8,128)} %copy-done.1, f32[384]{0:T(512)S(1)} %get-tuple-element.20, s32[384]{0:T(512)S(1)} %iota_add_fusion, s32[6144]{0:T(1024)S(1)} %bitcast.29, s32[384]{0:T(512)S(1)} %reduce, ...), kind=kOutput, calls=%fused_computation.16 | convolution fusion | flops 1423835136 | bytes 14643712 | tf_op jit(solution)/shard_map/dot_general | solution.py:22
  124.8 0.0 all-reduce.7.cloned.1.call-update
  124.9 0.0 all-reduce.5.cloned.1.call-start
  124.9 61.4 %all-reduce.7.cloned.1.call-done = (f32[1024,256]{0,1:T(8,128)}, f32[1024,256]{0,1:T(8,128)}) async-done(((f32[1024,256]{0,1:T(8,128)}, f32[1024,256]{0,1:T(8,128)}), (f32[1024,256]{0,1:T(8,128)}, f32[1024,256]{0,1:T(8,128)})) %all-reduce.7.cloned.1.call-update) | async-done | bytes 2097168 | tf_op jit(solution)/shard_map/psum | solution.py:11
  186.3 0.0 all-reduce.5.cloned.1.call-update
  186.3 5.6 %psum.46 = f32[]{:T(128)} all-reduce(f32[]{:T(128)} %get-tuple-element.19), channel_id=1, replica_groups=mesh['blk'=16,'dp'=2] {'dp'}, use_global_device_ids=true, to_apply=%region_8.9 | all-reduce | flops 1 | bytes 8 | tf_op jit(solution)/shard_map/psum | solution.py:11
  191.9 33.2 %psum.47 = f32[]{:T(128)} all-reduce(f32[]{:T(128)} %psum.46), channel_id=1, replica_groups=mesh['blk'=16,'dp'=2] {'blk'}, use_global_device_ids=true, to_apply=%region_9.10 | all-reduce | flops 1 | bytes 8 | tf_op jit(solution)/shard_map/psum | solution.py:12
  225.7 62.5 %all-reduce.5.cloned.1.call-done = (f32[1024,256]{0,1:T(8,128)}, f32[1024,256]{0,1:T(8,128)}) async-done(((f32[1024,256]{0,1:T(8,128)}, f32[1024,256]{0,1:T(8,128)}), (f32[1024,256]{0,1:T(8,128)}, f32[1024,256]{0,1:T(8,128)})) %all-reduce.5.cloned.1.call-update) | async-done | bytes 2097168 | tf_op jit(solution)/shard_map/psum | solution.py:12
  288.2 2.5 copy.16
  290.7 2.5 copy.17
  (3 shorter events, 0.0 us)
Async XLA Ops:
  7.2 1.1 copy-start
  7.2 52.3 %all-gather.6.cloned.1.call-start = ((), (), s32[]{:S(2)}) async-start(), calls=%async_computation | async-start | bytes 3342336 | tf_op jit(solution)/shard_map/all_gather | solution.py:40
  10.4 95.5 %all-gather.8.cloned.1.call-start = ((), (), s32[]{:S(2)}) async-start(), calls=%async_computation.1 | async-start | bytes 3342336 | tf_op jit(solution)/shard_map/all_gather | solution.py:71
  12.8 173.5 %all-reduce.7.cloned.1.call-start = ((), (), s32[]{:S(2)}) async-start(), calls=%async_computation.3 | async-start | bytes 4194304 | tf_op jit(solution)/shard_map/psum | solution.py:11
  64.6 3.6 %copy-start.1 = (f32[384,6144]{1,0:T(8,128)}, f32[384,6144]{1,0:T(8,128)S(1)}, u32[]{:S(2)}) copy-start(f32[384,6144]{1,0:T(8,128)S(1)} %get-tuple-element.22) | copy-start | bytes 28311556
  64.6 41.3 %copy-start.3 = (bf16[384,256]{1,0:T(8,128)(2,1)S(1)}, bf16[384,256]{1,0:T(8,128)(2,1)}, u32[]{:S(2)}) copy-start(bf16[384,256]{1,0:T(8,128)(2,1)} %convolution_convert_fusion) | copy-start | bytes 589828
  64.6 41.3 %copy-start.4 = (bf16[384,256]{1,0:T(8,128)(2,1)S(1)}, bf16[384,256]{1,0:T(8,128)(2,1)}, u32[]{:S(2)}) copy-start(bf16[384,256]{1,0:T(8,128)(2,1)} %convolution_convert_fusion.1) | copy-start | bytes 589828
  105.9 9.9 %copy-start.2 = (bf16[1,384,1024]{2,1,0:T(8,128)(2,1)S(1)}, bf16[1,384,1024]{2,1,0:T(8,128)(2,1)}, u32[]{:S(2)}) copy-start(bf16[1,384,1024]{2,1,0:T(8,128)(2,1)} %param.7) | copy-start | bytes 2359300
  124.9 163.3 %all-reduce.5.cloned.1.call-start = ((), (), s32[]{:S(2)}) async-start(), calls=%async_computation.2 | async-start | bytes 4194304 | tf_op jit(solution)/shard_map/psum | solution.py:12
Sparse Core Ops, SparseCore 0:
  10.8 48.2 all-gather.5
  62.0 43.8 all-gather.7
  125.0 61.2 all-reduce.6
  189.8 98.3 all-reduce.4
